TPU v7x, 256 devices: a whole 4x4x8 slice. The times are simulated.
256 devices in a mesh: dp: 32 (over z, x), mp: 8 (over y, core).
Axes of the slice: x: 4, y: 4, z: 8, core: 2. Of those that a mesh axis runs over, the one named last changes fastest.
Arguments:
- activations: bfloat16 [16384, 3072], P('dp', 'mp'), may hold values from -6 to 6
- out_grads: bfloat16 [16384, 6144], P('dp', 'mp'), may hold values from -0.25 to 0.25
- error: bfloat16 [32, 3072, 6144], P('dp', 'mp'), may hold values from -8 to 8
- sketch: bfloat16 [6144, 64], replicated, may hold values from -0.078125 to 0.078125
- momentum: float32 [3072, 6144], P('mp', 'dp'), may hold values from -6 to 6
Outputs:
- error_new: bfloat16 [32, 3072, 6144], P('dp', 'mp')
- momentum_new: float32 [3072, 6144], P('mp', 'dp')
- next_sketch: bfloat16 [6144, 64], replicated
All inputs are finite; a program needn't handle non-finite values.
Results may differ from a plain program's by a relative error of at most 0.0057.
Values may be sent and summed in bfloat16 or wider, within the bound.
No kernel may reach another device: no remote copies, remote signals or barrier semaphores. Data moves between devices by JAX's collectives and lax.ppermute only.
A program may use at most 64 MiB of HBM per device.

v0:
```python
import jax
import jax.numpy as jnp
from jax import lax
from jax.sharding import Mesh
from jax.sharding import PartitionSpec as P

MP = ("mp_0", "mp_1")
DP = ("dp_0", "dp_1")
beta_decay = 0.9


def cut_along(shard, dim, peers):
    before, after = (shard.shape[:dim], shard.shape[dim + 1 :])
    return jnp.moveaxis(shard.reshape(*before, peers, -1, *after), dim, 0)


def summed_on_arrival(shard, axis, dim):
    blocks = cut_along(shard, dim, lax.axis_size(axis))
    arrived = lax.all_to_all(blocks, axis, split_axis=0, concat_axis=0, tiled=True)
    return arrived.sum(axis=0)


def filled_up(lines, peers):
    spare = -lines.shape[0] % peers
    if not spare:
        return lines
    return jnp.concatenate([lines, jnp.zeros((spare, *lines.shape[1:]), lines.dtype)])


def in_order(blocks, dim):
    blocks = jnp.moveaxis(blocks, 0, dim)
    dims = blocks.shape
    return blocks.reshape(*dims[:dim], dims[dim] * dims[dim + 1], *dims[dim + 2 :])


def copy_for_each(shard, axis):
    copies = jnp.broadcast_to(shard, (lax.axis_size(axis), *shard.shape))
    return lax.all_to_all(copies, axis, split_axis=0, concat_axis=0, tiled=True)


def collect(shard, axis, dim):
    return in_order(copy_for_each(shard, axis), dim)


def nested_sum(shard, axes):
    lines = shard.reshape(-1, shard.shape[-1])
    own = summed_on_arrival(filled_up(lines, lax.axis_size(axes)), axes, 0)
    whole = collect(own, axes, 0)
    return whole[: len(lines)].reshape(shard.shape)


def over_copies(shard, axis):
    return copy_for_each(shard, axis).sum(axis=0)


def gathered_by_axis(shard, axes, dim):
    far, near = axes
    blocks = copy_for_each(copy_for_each(shard, far), near)
    return in_order(blocks.swapaxes(0, 1).reshape(-1, *shard.shape), dim)


def sum_in_two_steps(shard, axes, dim):
    far, near = axes
    own = summed_on_arrival(cut_along(shard, dim, lax.axis_size(far)), near, dim + 1)
    return jnp.sum(lax.all_to_all(own, far, 0, 0, tiled=True), axis=0)


def total_of(shard, axes):
    lines = shard.reshape(-1, shard.shape[-1])
    padded = filled_up(lines, lax.axis_size(axes[0]) * lax.axis_size(axes[1]))
    whole = gathered_by_axis(sum_in_two_steps(padded, axes, 0), axes, 0)
    return lax.slice_in_dim(whole, 0, len(lines)).reshape(shard.shape)


def update_momentum(momentum, basis_rows, sketch_block):
    product = lax.dot_general(
        basis_rows, sketch_block, (((1,), (1,)), ((), ())), preferred_element_type=jnp.float32
    )
    return beta_decay * momentum + product


def local(activations, out_grads, error, sketch, momentum):
    own_error = error[0]
    product = lax.dot_general(
        activations,
        lax.all_gather(out_grads, MP, axis=1, tiled=True),
        (((0,), (0,)), ((), ())),
        preferred_element_type=jnp.float32,
    )
    accumulated = (product + own_error.astype(jnp.float32)).astype(jnp.bfloat16)
    local_left = jnp.dot(accumulated, sketch, preferred_element_type=jnp.float32)
    left_sketch = nested_sum(local_left, DP)
    gram_local = jnp.dot(
        left_sketch.T,
        left_sketch,
        precision=lax.Precision.HIGHEST,
        preferred_element_type=jnp.float32,
    )
    gram_matrix = over_copies(gram_local, MP)
    factor = jnp.linalg.cholesky(gram_matrix)
    basis_rows = jax.scipy.linalg.solve_triangular(factor, left_sketch.T, lower=True).T.astype(
        jnp.bfloat16
    )
    block_width = momentum.shape[1]
    local_right = lax.dot_general(
        accumulated, basis_rows, (((0,), (0,)), ((), ())), preferred_element_type=jnp.float32
    )
    right_sketch = total_of(local_right, (("dp_0", "dp_1"), ("mp_0", "mp_1")))
    next_sketch = right_sketch.astype(jnp.bfloat16)
    sketch_part = lax.dynamic_slice_in_dim(
        next_sketch, lax.axis_index(DP) * block_width, block_width, 0
    )
    momentum_new = update_momentum(momentum, basis_rows, sketch_part)
    decoded = lax.dot_general(
        basis_rows, next_sketch, (((1,), (1,)), ((), ())), preferred_element_type=jnp.float32
    )
    error_new = (accumulated.astype(jnp.float32) - decoded / lax.axis_size(DP)).astype(jnp.bfloat16)
    return (error_new[None], momentum_new, next_sketch)


def solution(mesh):
    split = Mesh(mesh.devices.reshape(8, 4, 4, 2), ("dp_0", "dp_1", "mp_0", "mp_1"))
    placed = (P(DP, MP), P(DP, MP), P(DP, MP, None), P(), P(MP, DP))
    return jax.shard_map(
        local,
        mesh=split,
        in_specs=placed,
        out_specs=(P(DP, MP, None), P(MP, DP), P()),
        check_vma=False,
    )
```

profile of v0, /device:TPU:1, one launch (start us, length us, event | category | flops | bytes accessed | tf_op | source)
XLA Modules:
  0.0 240.9 jit_solution(73632805947021888)
XLA Ops:
  7.9 49.6 %all-gather.2.cloned.1.call-done = bf16[512,6144]{1,0:T(8,128)(2,1)} async-done(((bf16[512,768]{1,0:T(8,128)(2,1)}), bf16[512,6144]{1,0:T(8,128)(2,1)}) %all-gather.2.cloned.1.call-update) | async-done | bytes 6291472 | tf_op jit(solution)/shard_map/all_gather | solution.py:86
  57.5 6.9 %fusion = bf16[384,6144]{1,0:T(8,128)(2,1)S(1)} fusion(bf16[512,384]{1,0:T(8,128)(2,1)} %param.5, bf16[512,6144]{1,0:T(8,128)(2,1)} %all-gather.2.cloned.1.call-done, bf16[1,384,6144]{2,1,0:T(8,128)(2,1)} %param.7), kind=kOutput, calls=%fused_computation.1 | convolution fusion | flops 2422996992 | bytes 16121856 | tf_op jit(solution)/shard_map/dot_general | solution.py:84
  64.4 2.2 copy-done.1
  68.2 18.4 %all_to_all.35 = f32[32,1,768]{2,1,0:T(1,128)S(1)} all-to-all(f32[32,1,768]{2,1,0:T(1,128)S(1)} %reshape.29), channel_id=1, replica_groups=mesh['dp_0'=8,'dp_1'=4,'mp_0'=4,'mp_1'=2] {'dp_0','dp_1'}, dimensions={0} | all-to-all | bytes 196608 | tf_op jit(solution)/shard_map/all_to_all | solution.py:19
  88.3 12.3 %all_to_all.36 = f32[32,1,768]{2,1,0:T(1,128)S(1)} all-to-all(f32[32,1,768]{2,1,0:T(1,128)S(1)} %reshape.31), channel_id=1, replica_groups=mesh['dp_0'=8,'dp_1'=4,'mp_0'=4,'mp_1'=2] {'dp_0','dp_1'}, dimensions={0} | all-to-all | bytes 196608 | tf_op jit(solution)/shard_map/all_to_all | solution.py:38
  103.0 6.2 %all-to-all-start.2 = ((f32[8,1,4096]{2,1,0:T(1,128)}), f32[8,1,4096]{2,1,0:T(1,128)S(1)}, u32[]{:S(2)}, u32[]{:S(2)}) async-start(f32[8,1,4096]{2,1,0:T(1,128)} %reshape.33), calls=%async_computation.2 | async-start | bytes 262144 | tf_op jit(solution)/shard_map/all_to_all | solution.py:38
  109.2 5.2 %all-to-all-done.2 = f32[8,1,4096]{2,1,0:T(1,128)S(1)} async-done(((f32[8,1,4096]{2,1,0:T(1,128)}), f32[8,1,4096]{2,1,0:T(1,128)S(1)}, u32[]{:S(2)}, u32[]{:S(2)}) %all-to-all-start.2) | async-done | bytes 131104 | tf_op jit(solution)/shard_map/all_to_all | solution.py:38
  115.6 5.8 %cholesky.16 = f32[64,64]{1,0:T(8,128)S(1)} custom-call(f32[64,64]{1,0:T(8,128)S(1)} %fusion.6), custom_call_target="Cholesky" | custom-call | tf_op jit(solution)/shard_map/jit(cholesky)/cholesky | solution.py:100
  122.8 4.9 %custom-call.7 = f32[1,64,64]{1,2,0:T(8,128)S(1)} custom-call(f32[1,64,64]{2,1,0:T(8,128)S(1)} %fusion.4), custom_call_target="InvertDiagBlocksLowerTriangular" | custom-call | tf_op jit(solution)/shard_map/jit(_solve_triangular)/triangular_solve | solution.py:101
  128.2 3.8 %fusion.9 = f32[6144,64]{1,0:T(8,128)S(1)} fusion(bf16[384,6144]{1,0:T(8,128)(2,1)} %copy-done.1, bf16[384,64]{0,1:T(8,128)(2,1)S(1)} %convolution_convert_fusion), kind=kOutput, calls=%fused_computation.21 | convolution fusion | flops 301989888 | bytes 6340608 | tf_op jit(solution)/shard_map/dot_general | solution.py:105
  132.0 1.9 copy.27
  133.9 3.8 %reshape.35 = f32[8,1,49152]{2,1,0:T(1,128)S(1)} reshape(f32[8,32,24,64]{3,2,1,0:T(8,128)} %copy.27) | data formatting | bytes 3145728
  137.7 24.6 %all_to_all.37 = f32[8,1,49152]{2,1,0:T(1,128)} all-to-all(f32[8,1,49152]{2,1,0:T(1,128)S(1)} %reshape.35), channel_id=1, replica_groups=mesh['dp_0'=8,'dp_1'=4,'mp_0'=4,'mp_1'=2] {'mp_0','mp_1'}, dimensions={0} | all-to-all | bytes 3145728 | tf_op jit(solution)/shard_map/all_to_all | solution.py:19
  162.2 5.8 %reduce.9 = f32[8,49152]{1,0:T(8,128)S(1)} reduce(f32[8,1,49152]{2,1,0:T(1,128)} %all_to_all.37, f32[]{:T(128)} %broadcast.54), dimensions={1}, to_apply=%all_to_all.24.reduce_sub_computation | reduce | bytes 3145732 | tf_op jit(solution)/shard_map/all_to_all | solution.py:19
  168.0 2.9 %reshape.36 = f32[8,32,24,64]{3,2,1,0:T(8,128)} reshape(f32[8,49152]{1,0:T(8,128)S(1)} %reduce.9) | data formatting | bytes 3145728
  171.0 2.1 reduce_sum.38
  173.3 13.0 %all_to_all.38 = f32[32,1,1536]{2,1,0:T(1,128)S(1)} all-to-all(f32[32,1,1536]{2,1,0:T(1,128)S(1)} %reshape.37), channel_id=1, replica_groups=mesh['dp_0'=8,'dp_1'=4,'mp_0'=4,'mp_1'=2] {'dp_0','dp_1'}, dimensions={0} | all-to-all | bytes 393216 | tf_op jit(solution)/shard_map/all_to_all | solution.py:65
  187.8 12.9 %all_to_all.39 = bf16[32,2,768]{2,1,0:T(2,128)(2,1)S(1)} all-to-all(bf16[32,2,768]{2,1,0:T(2,128)(2,1)S(1)} %reshape.39), channel_id=1, replica_groups=mesh['dp_0'=8,'dp_1'=4,'mp_0'=4,'mp_1'=2] {'dp_0','dp_1'}, dimensions={0} | all-to-all | bytes 196608 | tf_op jit(solution)/shard_map/all_to_all | solution.py:38
  201.1 1.9 reshape.41
  203.0 6.9 %all-to-all-start.6 = ((bf16[8,2,24576]{2,1,0:T(2,128)(2,1)}), bf16[8,2,24576]{2,1,0:T(2,128)(2,1)S(1)}, u32[]{:S(2)}, u32[]{:S(2)}) async-start(bf16[8,2,24576]{2,1,0:T(2,128)(2,1)} %reshape.41), calls=%async_computation.6 | async-start | bytes 1572864 | tf_op jit(solution)/shard_map/all_to_all | solution.py:38
  209.9 12.2 %all-to-all-done.6 = bf16[8,2,24576]{2,1,0:T(2,128)(2,1)S(1)} async-done(((bf16[8,2,24576]{2,1,0:T(2,128)(2,1)}), bf16[8,2,24576]{2,1,0:T(2,128)(2,1)S(1)}, u32[]{:S(2)}, u32[]{:S(2)}) %all-to-all-start.6) | async-done | bytes 786464 | tf_op jit(solution)/shard_map/all_to_all | solution.py:38
  222.1 1.9 reshape.42
  224.0 1.8 copy.28
  225.8 6.0 %fusion.1 = bf16[1,384,6144]{2,1,0:T(8,128)(2,1)} fusion(bf16[384,64]{0,1:T(8,128)(2,1)S(1)} %convolution_convert_fusion, bf16[6144,64]{1,0:T(8,128)(2,1)S(1)} %bitcast.33, bf16[384,6144]{1,0:T(8,128)(2,1)} %copy-done.1), kind=kOutput, calls=%fused_computation.3 | convolution fusion | flops 311427072 | bytes 10272768 | tf_op jit(solution)/shard_map/dot_general | solution.py:114
  (41 shorter events, 13.6 us)
Async XLA Ops:
  7.2 59.5 %copy-start = (bf16[6144,64]{0,1:T(8,128)(2,1)S(1)}, bf16[6144,64]{0,1:T(8,128)(2,1)}, u32[]{:S(2)}) copy-start(bf16[6144,64]{0,1:T(8,128)(2,1)} %param.8) | copy-start | bytes 2359300
  7.2 50.3 %all-gather.2.cloned.1.call-start = ((), (), s32[]{:S(2)}) async-start(), calls=%async_computation.7 | async-start | bytes 7077888 | tf_op jit(solution)/shard_map/all_gather | solution.py:86
  64.4 2.2 copy-start.1
  103.0 11.5 %all-to-all-start.2 = ((f32[8,1,4096]{2,1,0:T(1,128)}), f32[8,1,4096]{2,1,0:T(1,128)S(1)}, u32[]{:S(2)}, u32[]{:S(2)}) async-start(f32[8,1,4096]{2,1,0:T(1,128)} %reshape.33), calls=%async_computation.2 | async-start | bytes 262144 | tf_op jit(solution)/shard_map/all_to_all | solution.py:38
  203.0 19.1 %all-to-all-start.6 = ((bf16[8,2,24576]{2,1,0:T(2,128)(2,1)}), bf16[8,2,24576]{2,1,0:T(2,128)(2,1)S(1)}, u32[]{:S(2)}, u32[]{:S(2)}) async-start(bf16[8,2,24576]{2,1,0:T(2,128)(2,1)} %reshape.41), calls=%async_computation.6 | async-start | bytes 1572864 | tf_op jit(solution)/shard_map/all_to_all | solution.py:38
  225.8 7.4 %copy-start.2 = (f32[384,192]{0,1:T(8,128)S(1)}, f32[384,192]{0,1:T(8,128)}, u32[]{:S(2)}) copy-start(f32[384,192]{0,1:T(8,128)} %param.9) | copy-start | bytes 884740
Sparse Core Ops, SparseCore 0:
  9.8 47.6 all-gather.1
where the time goes:
time: 242 us; the launch traced here: 241 us
  blocking collectives  81.1 us (34%)
  waiting for transfers between devices  67.7 us (28%)
  other arithmetic  23.9 us (10%)
  local copies, waits for them, and re-layouts  20.9 us (9%)
  matrix products  20 us (8%)
  between operations  14.3 us (6%)
  starting transfers between devices  13.1 us (5%)
    all_gather x1, waiting for transfers between devices, local(): lax.all_gather(out_grads, MP, axis=1, tiled=True)  49.6 us
    all_to_all x2, blocking collectives, summed_on_arrival(): lax.all_to_all(blocks, axis, split_axis=0, concat_axis=0, tiled=True)  43 us
    all_to_all x2, blocking collectives, copy_for_each(): return lax.all_to_all(copies, axis, split_axis=0, concat_axis=0, tiled=True)  25.2 us
    all_to_all x2, waiting for transfers between devices, copy_for_each(): return lax.all_to_all(copies, axis, split_axis=0, concat_axis=0, tiled=True)  17.4 us
    unnamed x21, local copies, waits for them, and re-layouts  16.3 us
    all_to_all x2, starting transfers between devices, copy_for_each(): return lax.all_to_all(copies, axis, split_axis=0, concat_axis=0, tiled=True)  13.1 us
    all_to_all x1, blocking collectives, sum_in_two_steps(): return jnp.sum(lax.all_to_all(own, far, 0, 0, tiled=True), axis=0)  13 us
    dot_general x1, matrix products, local(): lax.dot_general(activations, lax.all_gather(out_grads, MP, axis=1, tiled=...  6.95 us
  transfers between devices with their start and end apart: 3, of which 3 were waited for; matrix products, arithmetic and copies ran while one was open for 0% of the time, Pallas kernels for 0%

commit v1 on v0

--- a/solution.py
+++ b/solution.py
@@ -83,7 +83,9 @@
     own_error = error[0]
     product = lax.dot_general(
         activations,
-        lax.all_gather(out_grads, MP, axis=1, tiled=True),
+        jnp.concatenate(
+            lax.all_to_all(jnp.stack(lax.axis_size(MP) * [out_grads]), MP, 0, 0), axis=1
+        ),
         (((0,), (0,)), ((), ())),
         preferred_element_type=jnp.float32,
     )

time: 242 us -> 255 us (1.054)
  blocking collectives: 81.1 us -> 160 us
  waiting for transfers between devices: 67.7 us -> 17.4 us
  between operations: 14.3 us -> 0.92 us
  matrix products: 20 us -> 15.9 us
    all_to_all x0 -> x1, blocking collectives: none -> 77.1 us  [local(): lax.all_to_all(jnp.stack(lax.axis_size(MP) * [out_grads]), MP, 0, 0)]
    all_gather x1 -> x0, waiting for transfers between devices: 49.6 us -> none  [local(): lax.all_gather(out_grads, MP, axis=1, tiled=True)]
    dot_general x1, matrix products: 6.95 us -> 2.91 us  [local(): lax.dot_general(activations, jnp.concatenate(lax.all_to_all(jnp.stack(lax...]
    unnamed x21 -> x28, local copies, waits for them, and re-layouts: 16.3 us -> 17.8 us
  transfers between devices with their start and end apart: 3 -> 2, of which waited for: 3 -> 2; matrix products, arithmetic and copies ran while one was open for 0% -> 0% of each run, Pallas kernels for 0% -> 0%
where the time goes in v1:
time: 255 us
  blocking collectives  160 us (63%)
  other arithmetic  23.9 us (9%)
  local copies, waits for them, and re-layouts  22.9 us (9%)
  waiting for transfers between devices  17.4 us (7%)
  matrix products  15.9 us (6%)
  starting transfers between devices  13.8 us (5%)
    all_to_all x1, blocking collectives, local(): lax.all_to_all(jnp.stack(lax.axis_size(MP) * [out_grads]), MP, 0, 0)  77.1 us
    all_to_all x2, blocking collectives, summed_on_arrival(): lax.all_to_all(blocks, axis, split_axis=0, concat_axis=0, tiled=True)  44.5 us
    all_to_all x2, blocking collectives, copy_for_each(): return lax.all_to_all(copies, axis, split_axis=0, concat_axis=0, tiled=True)  25.2 us
    unnamed x28, local copies, waits for them, and re-layouts  17.8 us
    all_to_all x2, waiting for transfers between devices, copy_for_each(): return lax.all_to_all(copies, axis, split_axis=0, concat_axis=0, tiled=True)  17.4 us
    all_to_all x2, starting transfers between devices, copy_for_each(): return lax.all_to_all(copies, axis, split_axis=0, concat_axis=0, tiled=True)  13.8 us
    all_to_all x1, blocking collectives, sum_in_two_steps(): return jnp.sum(lax.all_to_all(own, far, 0, 0, tiled=True), axis=0)  13 us
    all_to_all x2, other arithmetic, summed_on_arrival(): lax.all_to_all(blocks, axis, split_axis=0, concat_axis=0, tiled=True)  6.67 us
  transfers between devices with their start and end apart: 2, of which 2 were waited for; matrix products, arithmetic and copies ran while one was open for 0% of the time, Pallas kernels for 0%

profile of v1, /device:TPU:1, one launch (start us, length us, event | category | flops | bytes accessed | tf_op | source)
XLA Modules:
  0.0 254.7 jit_solution(904935183737858082)
XLA Ops:
  2.7 77.1 %all_to_all.40 = bf16[8,512,768]{1,2,0:T(8,128)(2,1)S(1)} all-to-all(bf16[8,512,768]{1,2,0:T(8,128)(2,1)S(1)} %stack.2), channel_id=1, replica_groups=mesh['dp_0'=8,'dp_1'=4,'mp_0'=4,'mp_1'=2] {'mp_0','mp_1'}, dimensions={0} | all-to-all | bytes 12582912 | tf_op jit(solution)/shard_map/all_to_all | solution.py:87
  79.9 2.9 %fusion = bf16[384,6144]{1,0:T(8,128)(2,1)S(1)} fusion(bf16[512,384]{1,0:T(8,128)(2,1)S(1)} %copy-done.3, bf16[512,6144]{0,1:T(8,128)(2,1)S(1)} %bitcast.40, bf16[1,384,6144]{2,1,0:T(8,128)(2,1)S(1)} %bitcast.43), kind=kOutput, calls=%fused_computation.1 | convolution fusion | flops 2422996992 | bytes 16121856 | tf_op jit(solution)/shard_map/dot_general | solution.py:84
  82.8 2.2 copy-done.1
  86.5 19.9 %all_to_all.41 = f32[32,1,768]{2,1,0:T(1,128)S(1)} all-to-all(f32[32,1,768]{2,1,0:T(1,128)S(1)} %reshape.39), channel_id=1, replica_groups=mesh['dp_0'=8,'dp_1'=4,'mp_0'=4,'mp_1'=2] {'dp_0','dp_1'}, dimensions={0} | all-to-all | bytes 196608 | tf_op jit(solution)/shard_map/all_to_all | solution.py:19
  108.2 12.3 %all_to_all.42 = f32[32,1,768]{2,1,0:T(1,128)S(1)} all-to-all(f32[32,1,768]{2,1,0:T(1,128)S(1)} %reshape.41), channel_id=1, replica_groups=mesh['dp_0'=8,'dp_1'=4,'mp_0'=4,'mp_1'=2] {'dp_0','dp_1'}, dimensions={0} | all-to-all | bytes 196608 | tf_op jit(solution)/shard_map/all_to_all | solution.py:38
  122.8 6.9 %all-to-all-start.3 = ((f32[8,1,4096]{2,1,0:T(1,128)}), f32[8,1,4096]{2,1,0:T(1,128)S(1)}, u32[]{:S(2)}, u32[]{:S(2)}) async-start(f32[8,1,4096]{2,1,0:T(1,128)} %reshape.43), calls=%async_computation.3 | async-start | bytes 262144 | tf_op jit(solution)/shard_map/all_to_all | solution.py:38
  129.8 5.2 %all-to-all-done.3 = f32[8,1,4096]{2,1,0:T(1,128)S(1)} async-done(((f32[8,1,4096]{2,1,0:T(1,128)}), f32[8,1,4096]{2,1,0:T(1,128)S(1)}, u32[]{:S(2)}, u32[]{:S(2)}) %all-to-all-start.3) | async-done | bytes 131104 | tf_op jit(solution)/shard_map/all_to_all | solution.py:38
  136.2 5.8 %cholesky.16 = f32[64,64]{1,0:T(8,128)S(1)} custom-call(f32[64,64]{1,0:T(8,128)S(1)} %fusion.6), custom_call_target="Cholesky" | custom-call | tf_op jit(solution)/shard_map/jit(cholesky)/cholesky | solution.py:102
  143.4 4.9 %custom-call.7 = f32[1,64,64]{1,2,0:T(8,128)S(1)} custom-call(f32[1,64,64]{2,1,0:T(8,128)S(1)} %fusion.4), custom_call_target="InvertDiagBlocksLowerTriangular" | custom-call | tf_op jit(solution)/shard_map/jit(_solve_triangular)/triangular_solve | solution.py:103
  148.7 3.8 %fusion.9 = f32[6144,64]{1,0:T(8,128)S(1)} fusion(bf16[384,6144]{1,0:T(8,128)(2,1)} %copy-done.1, bf16[384,64]{0,1:T(8,128)(2,1)S(1)} %convolution_convert_fusion), kind=kOutput, calls=%fused_computation.21 | convolution fusion | flops 301989888 | bytes 6340608 | tf_op jit(solution)/shard_map/dot_general | solution.py:107
  152.6 1.9 copy.30
  154.4 3.8 %reshape.45 = f32[8,1,49152]{2,1,0:T(1,128)S(1)} reshape(f32[8,32,24,64]{3,2,1,0:T(8,128)} %copy.30) | data formatting | bytes 3145728
  158.3 24.6 %all_to_all.43 = f32[8,1,49152]{2,1,0:T(1,128)} all-to-all(f32[8,1,49152]{2,1,0:T(1,128)S(1)} %reshape.45), channel_id=1, replica_groups=mesh['dp_0'=8,'dp_1'=4,'mp_0'=4,'mp_1'=2] {'mp_0','mp_1'}, dimensions={0} | all-to-all | bytes 3145728 | tf_op jit(solution)/shard_map/all_to_all | solution.py:19
  182.8 5.8 %reduce.9 = f32[8,49152]{1,0:T(8,128)S(1)} reduce(f32[8,1,49152]{2,1,0:T(1,128)} %all_to_all.43, f32[]{:T(128)} %broadcast.56), dimensions={1}, to_apply=%all_to_all.28.reduce_sub_computation | reduce | bytes 3145732 | tf_op jit(solution)/shard_map/all_to_all | solution.py:19
  188.6 2.9 %reshape.46 = f32[8,32,24,64]{3,2,1,0:T(8,128)} reshape(f32[8,49152]{1,0:T(8,128)S(1)} %reduce.9) | data formatting | bytes 3145728
  191.5 2.1 reduce_sum.38
  193.9 13.0 %all_to_all.44 = f32[32,1,1536]{2,1,0:T(1,128)S(1)} all-to-all(f32[32,1,1536]{2,1,0:T(1,128)S(1)} %reshape.47), channel_id=1, replica_groups=mesh['dp_0'=8,'dp_1'=4,'mp_0'=4,'mp_1'=2] {'dp_0','dp_1'}, dimensions={0} | all-to-all | bytes 393216 | tf_op jit(solution)/shard_map/all_to_all | solution.py:65
  208.3 12.9 %all_to_all.45 = bf16[32,2,768]{2,1,0:T(2,128)(2,1)S(1)} all-to-all(bf16[32,2,768]{2,1,0:T(2,128)(2,1)S(1)} %reshape.49), channel_id=1, replica_groups=mesh['dp_0'=8,'dp_1'=4,'mp_0'=4,'mp_1'=2] {'dp_0','dp_1'}, dimensions={0} | all-to-all | bytes 196608 | tf_op jit(solution)/shard_map/all_to_all | solution.py:38
  221.7 1.9 reshape.51
  223.6 6.9 %all-to-all-start.7 = ((bf16[8,2,24576]{2,1,0:T(2,128)(2,1)}), bf16[8,2,24576]{2,1,0:T(2,128)(2,1)S(1)}, u32[]{:S(2)}, u32[]{:S(2)}) async-start(bf16[8,2,24576]{2,1,0:T(2,128)(2,1)} %reshape.51), calls=%async_computation.7 | async-start | bytes 1572864 | tf_op jit(solution)/shard_map/all_to_all | solution.py:38
  230.4 12.2 %all-to-all-done.7 = bf16[8,2,24576]{2,1,0:T(2,128)(2,1)S(1)} async-done(((bf16[8,2,24576]{2,1,0:T(2,128)(2,1)}), bf16[8,2,24576]{2,1,0:T(2,128)(2,1)S(1)}, u32[]{:S(2)}, u32[]{:S(2)}) %all-to-all-start.7) | async-done | bytes 786464 | tf_op jit(solution)/shard_map/all_to_all | solution.py:38
  242.6 1.9 reshape.52
  244.5 1.8 copy.31
  246.4 6.0 %fusion.1 = bf16[1,384,6144]{2,1,0:T(8,128)(2,1)} fusion(bf16[384,64]{0,1:T(8,128)(2,1)S(1)} %convolution_convert_fusion, bf16[6144,64]{1,0:T(8,128)(2,1)S(1)} %bitcast.36, bf16[384,6144]{1,0:T(8,128)(2,1)} %copy-done.1), kind=kOutput, calls=%fused_computation.3 | convolution fusion | flops 311427072 | bytes 10272768 | tf_op jit(solution)/shard_map/dot_general | solution.py:116
  (48 shorter events, 14.9 us)
Async XLA Ops:
  0.6 84.3 %copy-start = (bf16[6144,64]{0,1:T(8,128)(2,1)S(1)}, bf16[6144,64]{0,1:T(8,128)(2,1)}, u32[]{:S(2)}) copy-start(bf16[6144,64]{0,1:T(8,128)(2,1)} %param.8) | copy-start | bytes 2359300
  2.1 77.7 %slice-start = ((s8[4718592]{0:T(1024)(128)(4,1)}), s8[524288]{0:T(1024)(128)(4,1)S(1)}, s32[]{:S(2)}) async-start(s8[4718592]{0:T(1024)(128)(4,1)} %bitcast.42), calls=%async_computation.8 | async-start | bytes 1048576
  2.7 77.2 %slice-start.1 = ((s8[4718592]{0:T(1024)(128)(4,1)}), s8[4194304]{0:T(1024)(128)(4,1)S(1)}, s32[]{:S(2)}) async-start(s8[4718592]{0:T(1024)(128)(4,1)} %bitcast.42), calls=%async_computation.9 | async-start | bytes 8388608
  2.7 77.2 %copy-start.3 = (bf16[512,384]{1,0:T(8,128)(2,1)S(1)}, bf16[512,384]{1,0:T(8,128)(2,1)}, u32[]{:S(2)}) copy-start(bf16[512,384]{1,0:T(8,128)(2,1)} %param.5) | copy-start | bytes 1179652
  82.8 2.2 copy-start.1
  122.8 12.2 %all-to-all-start.3 = ((f32[8,1,4096]{2,1,0:T(1,128)}), f32[8,1,4096]{2,1,0:T(1,128)S(1)}, u32[]{:S(2)}, u32[]{:S(2)}) async-start(f32[8,1,4096]{2,1,0:T(1,128)} %reshape.43), calls=%async_computation.3 | async-start | bytes 262144 | tf_op jit(solution)/shard_map/all_to_all | solution.py:38
  223.6 19.1 %all-to-all-start.7 = ((bf16[8,2,24576]{2,1,0:T(2,128)(2,1)}), bf16[8,2,24576]{2,1,0:T(2,128)(2,1)S(1)}, u32[]{:S(2)}, u32[]{:S(2)}) async-start(bf16[8,2,24576]{2,1,0:T(2,128)(2,1)} %reshape.51), calls=%async_computation.7 | async-start | bytes 1572864 | tf_op jit(solution)/shard_map/all_to_all | solution.py:38
  246.4 7.4 %copy-start.2 = (f32[384,192]{0,1:T(8,128)S(1)}, f32[384,192]{0,1:T(8,128)}, u32[]{:S(2)}) copy-start(f32[384,192]{0,1:T(8,128)} %param.9) | copy-start | bytes 884740
